TPU v7x, 32 devices: a whole 2x2x4 slice. The times are simulated.
32 devices in a mesh: rep: 4 (over z), ep: 8 (over y, x, core).
Axes of the slice: x: 2, y: 2, z: 4, core: 2. Of those that a mesh axis runs over, the one named last changes fastest.
Arguments:
- tokens: bfloat16 [32, 256, 2048], P('rep', 'ep'), may hold values from -6 to 6
- cotangent: bfloat16 [32, 256, 2048], P('rep', 'ep'), may hold values from -6 to 6
- gate_weights: bfloat16 [32, 256, 8], P('rep', 'ep'), may hold values from 0.049804688 to 0.25
- expert_ids: int32 [32, 256, 8], P('rep', 'ep'), may hold values from 0 to 15, all different within a row; in each aligned block of 256 rows (0 to 255, 256 to 511, ..., all dimensions but the last counted through in order) at most 144 rows name the same one
- seq_lengths: int32 [32], P(('rep', 'ep')), may hold values from 1 to 256, 5120 in all
- query_weight: bfloat16 [2048, 2048], P('ep'), may hold values from -0.125 to 0.125
- key_weight: bfloat16 [2048, 2048], P('ep'), may hold values from -0.125 to 0.125
- value_weight: bfloat16 [2048, 2048], P('ep'), may hold values from -0.125 to 0.125
- output_weight: bfloat16 [2048, 2048], P('ep'), may hold values from -0.75 to 0.75
- attn_gain: bfloat16 [2048], P('ep'), may hold values from 0.25 to 1.75
- ffn_gain: bfloat16 [2048], P('ep'), may hold values from 0.25 to 1.75
- query_gain: bfloat16 [128], P('ep'), may hold values from 0.25 to 1.75
- key_gain: bfloat16 [128], P('ep'), may hold values from 0.25 to 1.75
- expert_in: bfloat16 [16, 2048, 2048], P('ep'), may hold values from -0.125 to 0.125
- expert_out: bfloat16 [16, 1024, 2048], P('ep'), may hold values from -0.5 to 0.5
Outputs:
- result: bfloat16 [32, 256, 2048], P('rep', 'ep')
- token_grad: bfloat16 [32, 256, 2048], P('rep', 'ep')
- query_weight_grad: float32 [2048, 2048], P('ep')
- key_weight_grad: float32 [2048, 2048], P('ep')
- value_weight_grad: float32 [2048, 2048], P('ep')
- output_weight_grad: float32 [2048, 2048], P('ep')
- attn_gain_grad: float32 [2048], P('ep')
- ffn_gain_grad: float32 [2048], P('ep')
- query_gain_grad: float32 [128], P('ep')
- key_gain_grad: float32 [128], P('ep')
- expert_in_grad: float32 [16, 2048, 2048], P('ep', 'rep')
- expert_out_grad: float32 [16, 1024, 2048], P('ep', 'rep')
Inputs may be any that keep to these rules, and one draw needn't show every extreme that they name: `expert_ids`: each token names 8 different experts; within the 256 token slots of one sequence no expert is named more than 144 times, and some expert of some sequence is named exactly 144 times. `seq_lengths`: some sequence is full, with exactly 256 live tokens; live tokens come first in a sequence.
All inputs are finite; a program needn't handle non-finite values. No bound on the sum of `seq_lengths` on one device may be relied on, other than what follows from the above.
Results may differ from a plain program's by a relative error of at most 0.028.
Values may be sent and summed in bfloat16 or wider, within the bound.
A program may use at most 320 MiB of HBM per device.

v0:
```python
import jax
import jax.numpy as jnp
from jax import lax
from jax.sharding import PartitionSpec as P

HEADS = 16
HEAD_DIM = 128
epsilon = 1e-06
rope_base = 50000.0


def rms_norm(values, gain_vector):
    return (
        values
        * lax.rsqrt(jnp.mean(values * values, axis=-1, keepdims=True) + epsilon)
        * gain_vector
    )


def rotary_tables(length, head_width):
    half_width = head_width // 2
    frequency = rope_base ** (-(jnp.arange(half_width, dtype=jnp.float32) * (2.0 / head_width)))
    angles = jnp.arange(length, dtype=jnp.float32)[:, None] * frequency[None, :]
    angles = jnp.concatenate([angles, angles], axis=-1)
    return (jnp.cos(angles)[:, None, :], jnp.sin(angles)[:, None, :])


def rotate(values, cos_table, sin_table):
    half_width = values.shape[-1] // 2
    turned = jnp.concatenate([-values[..., half_width:], values[..., :half_width]], axis=-1)
    return values * cos_table + turned * sin_table


def slot_index(expert_ids, experts, capacity):
    flat_ids = expert_ids.reshape(-1)
    choose = (flat_ids[:, None] == jnp.arange(experts, dtype=jnp.int32)[None, :]).astype(jnp.int32)
    before = jnp.cumsum(choose, axis=0) - choose
    ranking = jnp.sum(before * choose, axis=1)
    return flat_ids * capacity + ranking


def contract(left_side, right_side, left_dim, right_dim):
    return lax.dot_general(
        left_side,
        right_side,
        (((left_dim,), (right_dim,)), ((), ())),
        preferred_element_type=jnp.float32,
    )


def masked_scores(query_low, key_low, living, score_scale):
    raw_scores = (
        jnp.einsum("qhd,khd->hqk", query_low, key_low, preferred_element_type=jnp.float32)
        * score_scale
    )
    return jnp.where(living[None, None, :] > 0.5, raw_scores, -1000000000.0)


def shards(
    tokens,
    cotangent,
    gate_weights,
    expert_ids,
    seq_lengths,
    query_weight,
    key_weight,
    value_weight,
    output_weight,
    attn_gain,
    ffn_gain,
    query_gain,
    key_gain,
    expert_in,
    expert_out,
):
    ep_count = lax.axis_size("ep")
    dealt_arrays = (
        lax.all_to_all(tokens, "ep", split_axis=0, concat_axis=1, tiled=True),
        lax.all_to_all(cotangent, "ep", split_axis=0, concat_axis=1, tiled=True),
        lax.all_to_all(gate_weights, "ep", split_axis=0, concat_axis=1, tiled=True),
    )
    seq_tokens = dealt_arrays[0][0]
    seq_cot = dealt_arrays[1][0]
    seq_gates = dealt_arrays[2][0]
    seq_ids = lax.all_to_all(expert_ids, "ep", split_axis=0, concat_axis=1, tiled=True)[0]
    length = seq_tokens.shape[0]
    model_width = seq_tokens.shape[1]
    top_count = seq_gates.shape[1]
    local_experts = expert_in.shape[0]
    hidden_size = expert_out.shape[1]
    experts = local_experts * ep_count
    capacity = length * top_count * 9 // (8 * experts)
    score_scale = HEAD_DIM ** (-0.5)
    gathered_weights = (
        lax.all_gather(query_weight, "ep", axis=0, tiled=True),
        lax.all_gather(key_weight, "ep", axis=0, tiled=True),
        lax.all_gather(value_weight, "ep", axis=0, tiled=True),
        lax.all_gather(output_weight, "ep", axis=0, tiled=True),
        lax.all_gather(attn_gain, "ep", axis=0, tiled=True),
        lax.all_gather(ffn_gain, "ep", axis=0, tiled=True),
        lax.all_gather(query_gain, "ep", axis=0, tiled=True),
        lax.all_gather(key_gain, "ep", axis=0, tiled=True),
    )
    w_query = gathered_weights[0]
    w_key = gathered_weights[1]
    w_value = gathered_weights[2]
    w_output = gathered_weights[3]
    gain_attn = gathered_weights[4].astype(jnp.float32)
    gain_ffn = gathered_weights[5].astype(jnp.float32)
    gain_query = gathered_weights[6].astype(jnp.float32)
    gain_key = gathered_weights[7].astype(jnp.float32)
    positions = jnp.arange(length, dtype=jnp.int32)
    living = (positions < seq_lengths[0]).astype(jnp.float32)
    combine_weight = seq_gates.astype(jnp.float32) * living[:, None]
    destination = slot_index(seq_ids, experts, capacity)
    pair_count = length * top_count
    token_of_slot = (
        jnp.zeros((experts * capacity,), jnp.int32)
        .at[destination]
        .set(jnp.arange(pair_count, dtype=jnp.int32) // top_count)
    )
    slot_weight = (
        jnp.zeros((experts * capacity,), jnp.float32)
        .at[destination]
        .set(combine_weight.reshape(-1))
    )
    slot_filled = (
        jnp.zeros((experts * capacity,), jnp.bfloat16)
        .at[destination]
        .set(jnp.ones((pair_count,), jnp.bfloat16))
    )
    cos_table, sin_table = rotary_tables(length, HEAD_DIM)

    def head_piece(inputs_pre, gain_vector):
        return rotate(rms_norm(inputs_pre, gain_vector), cos_table, sin_table)

    residual_in = seq_tokens.astype(jnp.float32)
    normed = rms_norm(residual_in, gain_attn).astype(jnp.bfloat16)
    query_pre = jnp.dot(normed, w_query, preferred_element_type=jnp.float32).reshape(
        length, HEADS, HEAD_DIM
    )
    key_pre = jnp.dot(normed, w_key, preferred_element_type=jnp.float32).reshape(
        length, HEADS, HEAD_DIM
    )
    value_low = (
        jnp.dot(normed, w_value, preferred_element_type=jnp.float32)
        .astype(jnp.bfloat16)
        .reshape(length, HEADS, HEAD_DIM)
    )
    query_rot, query_pull = jax.vjp(head_piece, query_pre, gain_query)
    key_rot, key_pull = jax.vjp(head_piece, key_pre, gain_key)
    query_low = query_rot.astype(jnp.bfloat16)
    key_low = key_rot.astype(jnp.bfloat16)
    scores = masked_scores(query_low, key_low, living, score_scale)
    log_total = jax.nn.logsumexp(scores, axis=-1, keepdims=True)
    attention_low = jnp.exp(scores - log_total).astype(jnp.bfloat16)
    context = jnp.einsum(
        "hqk,khd->qhd", attention_low, value_low, preferred_element_type=jnp.float32
    )
    context = context.astype(jnp.bfloat16).reshape(length, HEADS * HEAD_DIM)
    attended = jnp.dot(context, w_output, preferred_element_type=jnp.float32) * living[:, None]
    middle = residual_in + attended
    mixed_in = rms_norm(middle, gain_ffn).astype(jnp.bfloat16)
    outgoing = (mixed_in[token_of_slot] * slot_filled[:, None]).reshape(
        ep_count, local_experts, capacity, model_width
    )
    arrived = lax.all_to_all(outgoing, "ep", split_axis=0, concat_axis=2, tiled=True)[0]
    gate_up = jnp.einsum("erd,edf->erf", arrived, expert_in, preferred_element_type=jnp.float32)

    def swiglu(paired):
        return jax.nn.silu(paired[..., :hidden_size]) * paired[..., hidden_size:]

    activated, swiglu_pull = jax.vjp(swiglu, gate_up)
    activated_low = activated.astype(jnp.bfloat16)
    produced = jnp.einsum(
        "erf,efd->erd", activated_low, expert_out, preferred_element_type=jnp.float32
    ).astype(jnp.bfloat16)
    returned = lax.all_to_all(
        produced[None], "ep", split_axis=2, concat_axis=0, tiled=True
    ).reshape(experts * capacity, model_width)
    gathered = returned[destination].reshape(length, top_count, model_width).astype(jnp.float32)
    outcome = middle + jnp.sum(combine_weight[:, :, None] * gathered, axis=1)
    upstream = seq_cot.astype(jnp.float32)
    outgoing_grad = (upstream[token_of_slot] * slot_weight[:, None]).astype(jnp.bfloat16)
    outgoing_grad = outgoing_grad.reshape(ep_count, local_experts, capacity, model_width)
    arrived_grad = lax.all_to_all(outgoing_grad, "ep", split_axis=0, concat_axis=2, tiled=True)[0]
    activated_grad = jnp.einsum(
        "erd,efd->erf", arrived_grad, expert_out, preferred_element_type=jnp.float32
    )
    gate_up_grad = swiglu_pull(activated_grad)[0].astype(jnp.bfloat16)
    out_local_grad = jnp.einsum(
        "erf,erd->efd", activated_low, arrived_grad, preferred_element_type=jnp.float32
    )
    in_local_grad = jnp.einsum(
        "erd,erf->edf", arrived, gate_up_grad, preferred_element_type=jnp.float32
    )
    arrived_back = jnp.einsum(
        "erf,edf->erd", gate_up_grad, expert_in, preferred_element_type=jnp.float32
    ).astype(jnp.bfloat16)
    expert_sums = (
        lax.psum_scatter(
            in_local_grad.astype(jnp.bfloat16), "rep", scatter_dimension=1, tiled=True
        ).astype(jnp.float32),
        lax.psum_scatter(
            out_local_grad.astype(jnp.bfloat16), "rep", scatter_dimension=1, tiled=True
        ).astype(jnp.float32),
    )
    returned_grad = lax.all_to_all(
        arrived_back[None], "ep", split_axis=2, concat_axis=0, tiled=True
    ).reshape(experts * capacity, model_width)
    mixed_grad = jnp.sum(
        returned_grad[destination].reshape(length, top_count, model_width).astype(jnp.float32),
        axis=1,
    )
    ffn_values, ffn_pull = jax.vjp(rms_norm, middle, gain_ffn)
    middle_part, ffn_gain_grad = ffn_pull(mixed_grad)
    middle_grad = upstream + middle_part
    attended_grad = (middle_grad * living[:, None]).astype(jnp.bfloat16)
    output_weight_grad = contract(context, attended_grad, 0, 0)
    context_grad = (
        contract(attended_grad, w_output, 1, 1)
        .astype(jnp.bfloat16)
        .reshape(length, HEADS, HEAD_DIM)
    )
    attention_again = jnp.exp(masked_scores(query_low, key_low, living, score_scale) - log_total)
    attention_again_low = attention_again.astype(jnp.bfloat16)
    value_grad = jnp.einsum(
        "hqk,qhd->khd", attention_again_low, context_grad, preferred_element_type=jnp.float32
    )
    value_grad = value_grad.astype(jnp.bfloat16).reshape(length, HEADS * HEAD_DIM)
    prob_grad = jnp.einsum(
        "qhd,khd->hqk", context_grad, value_low, preferred_element_type=jnp.float32
    )
    score_grad = attention_again * (
        prob_grad - jnp.sum(attention_again * prob_grad, axis=-1, keepdims=True)
    )
    score_grad = score_grad.astype(jnp.bfloat16)
    query_rot_grad = (
        jnp.einsum("hqk,khd->qhd", score_grad, key_low, preferred_element_type=jnp.float32)
        * score_scale
    )
    key_rot_grad = (
        jnp.einsum("hqk,qhd->khd", score_grad, query_low, preferred_element_type=jnp.float32)
        * score_scale
    )
    query_grad, query_gain_grad = query_pull(query_rot_grad)
    key_grad, key_gain_grad = key_pull(key_rot_grad)
    query_grad = query_grad.astype(jnp.bfloat16).reshape(length, HEADS * HEAD_DIM)
    key_grad = key_grad.astype(jnp.bfloat16).reshape(length, HEADS * HEAD_DIM)
    normed_grad = (
        contract(query_grad, w_query, 1, 1)
        + contract(key_grad, w_key, 1, 1)
        + contract(value_grad, w_value, 1, 1)
    )
    query_weight_grad = contract(normed, query_grad, 0, 0)
    key_weight_grad = contract(normed, key_grad, 0, 0)
    value_weight_grad = contract(normed, value_grad, 0, 0)
    attn_values, attn_pull = jax.vjp(rms_norm, residual_in, gain_attn)
    input_part, attn_gain_grad = attn_pull(normed_grad)
    input_grad = (middle_grad + input_part).astype(jnp.bfloat16)
    moved_back = (
        lax.all_to_all(
            outcome.astype(jnp.bfloat16)[None], "ep", split_axis=1, concat_axis=0, tiled=True
        ),
        lax.all_to_all(input_grad[None], "ep", split_axis=1, concat_axis=0, tiled=True),
    )
    shares = (
        lax.psum_scatter(
            query_weight_grad.astype(jnp.bfloat16), "ep", scatter_dimension=0, tiled=True
        ).astype(jnp.float32),
        lax.psum_scatter(
            key_weight_grad.astype(jnp.bfloat16), "ep", scatter_dimension=0, tiled=True
        ).astype(jnp.float32),
        lax.psum_scatter(
            value_weight_grad.astype(jnp.bfloat16), "ep", scatter_dimension=0, tiled=True
        ).astype(jnp.float32),
        lax.psum_scatter(
            output_weight_grad.astype(jnp.bfloat16), "ep", scatter_dimension=0, tiled=True
        ).astype(jnp.float32),
        lax.psum_scatter(
            attn_gain_grad.astype(jnp.bfloat16), "ep", scatter_dimension=0, tiled=True
        ).astype(jnp.float32),
        lax.psum_scatter(
            ffn_gain_grad.astype(jnp.bfloat16), "ep", scatter_dimension=0, tiled=True
        ).astype(jnp.float32),
        lax.psum_scatter(
            query_gain_grad.astype(jnp.bfloat16), "ep", scatter_dimension=0, tiled=True
        ).astype(jnp.float32),
        lax.psum_scatter(
            key_gain_grad.astype(jnp.bfloat16), "ep", scatter_dimension=0, tiled=True
        ).astype(jnp.float32),
    )
    shares = (
        lax.psum(shares[0].astype(jnp.bfloat16), "rep").astype(jnp.float32),
        lax.psum(shares[1].astype(jnp.bfloat16), "rep").astype(jnp.float32),
        lax.psum(shares[2].astype(jnp.bfloat16), "rep").astype(jnp.float32),
        lax.psum(shares[3].astype(jnp.bfloat16), "rep").astype(jnp.float32),
        lax.psum(shares[4].astype(jnp.bfloat16), "rep").astype(jnp.float32),
        lax.psum(shares[5].astype(jnp.bfloat16), "rep").astype(jnp.float32),
        lax.psum(shares[6].astype(jnp.bfloat16), "rep").astype(jnp.float32),
        lax.psum(shares[7].astype(jnp.bfloat16), "rep").astype(jnp.float32),
    )
    return (
        moved_back[0],
        moved_back[1],
        shares[0],
        shares[1],
        shares[2],
        shares[3],
        shares[4],
        shares[5],
        shares[6],
        shares[7],
        expert_sums[0],
        expert_sums[1],
    )


def solution(mesh):
    return jax.shard_map(
        shards,
        mesh=mesh,
        in_specs=(
            P("rep", "ep", None),
            P("rep", "ep", None),
            P("rep", "ep", None),
            P("rep", "ep", None),
            P(("rep", "ep")),
            P("ep", None),
            P("ep", None),
            P("ep", None),
            P("ep", None),
            P("ep"),
            P("ep"),
            P("ep"),
            P("ep"),
            P("ep", None, None),
            P("ep", None, None),
        ),
        out_specs=(
            P("rep", "ep", None),
            P("rep", "ep", None),
            P("ep", None),
            P("ep", None),
            P("ep", None),
            P("ep", None),
            P("ep"),
            P("ep"),
            P("ep"),
            P("ep"),
            P("ep", "rep", None),
            P("ep", "rep", None),
        ),
        check_vma=False,
    )
```

profile of v0, /device:TPU:0, one launch (start us, length us, event | category | flops | bytes accessed | tf_op | source)
XLA Modules:
  0.0 1802.4 jit_solution(4447141272363571093)
XLA Ops:
  90.3 14.6 scatter_custom_fusion.1
  183.2 71.8 %all-gather.7.cloned.1.call-done = bf16[2048,2048]{1,0:T(8,128)(2,1)} async-done(((bf16[256,2048]{1,0:T(8,128)(2,1)}), bf16[2048,2048]{1,0:T(8,128)(2,1)}) %all-gather.7.cloned.1.call-update) | async-done | bytes 8388624 | tf_op jit(solution)/shard_map/all_gather | solution.py:97
  263.1 66.4 %all-gather.13.cloned.1.call-done = bf16[2048,2048]{1,0:T(8,128)(2,1)} async-done(((bf16[256,2048]{1,0:T(8,128)(2,1)}), bf16[2048,2048]{1,0:T(8,128)(2,1)}) %all-gather.13.cloned.1.call-update) | async-done | bytes 8388624 | tf_op jit(solution)/shard_map/all_gather | solution.py:98
  329.5 15.4 multiply_reduce_fusion.7
  378.7 96.1 %all-to-all-done.3 = bf16[8,2,144,2048]{3,2,1,0:T(8,128)(2,1)} async-done(((bf16[8,2,144,2048]{3,2,1,0:T(8,128)(2,1)}), bf16[8,2,144,2048]{3,2,1,0:T(8,128)(2,1)}, u32[]{:S(2)}, u32[]{:S(2)}) %all-to-all-start.3) | async-done | bytes 9437216 | tf_op jit(solution)/shard_map/all_to_all | solution.py:167
  484.0 27.4 %fusion.66 = f32[2,1152,2048]{2,1,0:T(8,128)} fusion(bf16[2,1152,2048]{2,1,0:T(8,128)(2,1)} %bitcast.188, bf16[2,2048,2048]{2,1,0:T(8,128)(2,1)} %param.28), kind=kOutput, calls=%fused_computation.165 | convolution fusion | flops 19327352832 | bytes 45088768 | tf_op jit(solution)/shard_map/erd,edf->erf/dot_general | solution.py:168
  511.4 27.5 %fusion.31 = (f32[2,1152,1024]{2,1,0:T(8,128)}, f32[2,1152,1024]{2,1,0:T(8,128)}, bf16[2,1152,1024]{2,1,0:T(8,128)(2,1)}) fusion(f32[2,1152,2048]{2,1,0:T(8,128)} %fusion.66, bf16[2,1152,2048]{2,1,0:T(8,128)(2,1)} %bitcast.190, bf16[2,1024,2048]{2,1,0:T(8,128)(2,1)} %param.29), kind=kOutput, calls=%fused_computation.95 | convolution fusion | flops 9696706560 | bytes 60293120 | tf_op jit(solution)/shard_map/erd,efd->erf/dot_general | solution.py:187
  538.8 14.6 fusion.4
  553.5 27.9 %copy.113 = bf16[1,2,1152,2048]{3,1,0,2:T(2,128)(2,1)} copy(bf16[1,2,1152,2048]{3,2,1,0:T(8,128)(2,1)S(1)} %fusion.4) | data formatting | bytes 18874368 | tf_op jit(solution)/shard_map/broadcast_in_dim | solution.py:179
  586.5 27.6 %fusion.5 = bf16[1,2,1152,2048]{3,2,1,0:T(8,128)(2,1)} fusion(bf16[2,2048,2048]{2,1,0:T(8,128)(2,1)} %param.28, f32[2,1152,1024]{2,1,0:T(8,128)} %get-tuple-element.37, f32[2,1152,1024]{2,1,0:T(8,128)} %get-tuple-element.36), kind=kOutput, calls=%fused_computation.22 | convolution fusion | flops 19341508608 | bytes 45088768 | tf_op jit(solution)/shard_map/erf,edf->erd/dot_general | solution.py:197
  614.1 18.2 %copy.119 = bf16[1,2,1152,2048]{3,1,0,2:T(2,128)(2,1)} copy(bf16[1,2,1152,2048]{3,2,1,0:T(8,128)(2,1)} %fusion.5) | data formatting | bytes 18874368 | tf_op jit(solution)/shard_map/broadcast_in_dim | solution.py:209
  632.3 59.5 %all-to-all-done.4 = bf16[1,2,1152,2048]{3,1,0,2:T(2,128)(2,1)} async-done(((bf16[1,2,1152,2048]{3,1,0,2:T(2,128)(2,1)}), bf16[1,2,1152,2048]{3,1,0,2:T(2,128)(2,1)}, u32[]{:S(2)}, u32[]{:S(2)}) %all-to-all-start.4) | async-done | bytes 9437216 | tf_op jit(solution)/shard_map/all_to_all | solution.py:178
  709.0 93.1 %all-to-all-done.8 = bf16[1,2,1152,2048]{3,1,0,2:T(2,128)(2,1)} async-done(((bf16[1,2,1152,2048]{3,1,0,2:T(2,128)(2,1)}), bf16[1,2,1152,2048]{3,1,0,2:T(2,128)(2,1)}, u32[]{:S(2)}, u32[]{:S(2)}) %all-to-all-start.8) | async-done | bytes 9437216 | tf_op jit(solution)/shard_map/all_to_all | solution.py:208
  813.9 21.2 %gather_fusion.1 = bf16[2048,2048]{1,0:T(8,128)(2,1)} fusion(bf16[2304,2048]{1,0:T(8,128)(2,1)} %bitcast.178, s32[2048]{0:T(1024)S(1)} %broadcast_clamp_fusion), kind=kCustom, calls=%fused_computation.1 | custom fusion | bytes 16785408 | tf_op jit(solution)/shard_map/gather | solution.py:181
  835.1 21.4 %gather_fusion.3 = bf16[2048,2048]{1,0:T(8,128)(2,1)} fusion(bf16[2304,2048]{1,0:T(8,128)(2,1)} %bitcast.179, s32[2048]{0:T(1024)S(1)} %broadcast_clamp_fusion), kind=kCustom, calls=%fused_computation.3 | custom fusion | bytes 16785408 | tf_op jit(solution)/shard_map/gather | solution.py:212
  947.4 17.9 convolution_convert_fusion.7
  976.2 74.9 %reduce-scatter.13.cloned.1.call-done = bf16[256,2048]{1,0:T(8,128)(2,1)} async-done(((bf16[2048,2048]{1,0:T(8,128)(2,1)}), bf16[256,2048]{1,0:T(8,128)(2,1)}) %reduce-scatter.13.cloned.1.call-update) | async-done | bytes 1048592 | tf_op jit(solution)/shard_map/reduce_scatter | solution.py:277
  1051.0 75.0 %reduce-scatter.9.cloned.1.call-done = bf16[256,2048]{1,0:T(8,128)(2,1)} async-done(((bf16[2048,2048]{1,0:T(8,128)(2,1)}), bf16[256,2048]{1,0:T(8,128)(2,1)}) %reduce-scatter.9.cloned.1.call-update) | async-done | bytes 1048592 | tf_op jit(solution)/shard_map/reduce_scatter | solution.py:271
  1126.0 75.6 %reduce-scatter.7.cloned.1.call-done = bf16[256,2048]{1,0:T(8,128)(2,1)} async-done(((bf16[2048,2048]{1,0:T(8,128)(2,1)}), bf16[256,2048]{1,0:T(8,128)(2,1)}) %reduce-scatter.7.cloned.1.call-update) | async-done | bytes 1048592 | tf_op jit(solution)/shard_map/reduce_scatter | solution.py:268
  1201.7 29.4 %convolution_convert_fusion = bf16[2,2048,2048]{2,1,0:T(8,128)(2,1)} fusion(bf16[2,1152,2048]{2,1,0:T(8,128)(2,1)} %bitcast.189, f32[2,1152,1024]{2,1,0:T(8,128)} %get-tuple-element.37, f32[2,1152,1024]{2,1,0:T(8,128)} %get-tuple-element.36), kind=kOutput, calls=%fused_computation.13 | convolution fusion | flops 19345178624 | bytes 45088768 | tf_op jit(solution)/shard_map/erd,erf->edf/dot_general | solution.py:194
  1285.0 21.1 %all-reduce.12 = (bf16[2048]{0:T(1024)(128)(2,1)S(1)}, bf16[2048]{0:T(1024)(128)(2,1)S(1)}, bf16[128]{0:T(256)(128)(2,1)S(1)}, bf16[128]{0:T(256)(128)(2,1)S(1)}) all-reduce(bf16[2048]{0:T(1024)(128)(2,1)S(1)} %get-tuple-element.18, bf16[2048]{0:T(1024)(128)(2,1)S(1)} %get-tuple-element.16, ...), channel_id=6, replica_groups=mesh['rep'=4,'ep'=8] {'ep'}, use_global_device_ids=true, to_apply=%region_28.29.clone | all-reduce | flops 4352 | bytes 17408
  1329.6 19.3 %reduce-scatter.17.cloned.1.call-done = bf16[2,256,2048]{2,1,0:T(8,128)(2,1)} async-done(((bf16[2,1024,2048]{2,1,0:T(8,128)(2,1)}), bf16[2,256,2048]{2,1,0:T(8,128)(2,1)}) %reduce-scatter.17.cloned.1.call-update) | async-done | bytes 2097168 | tf_op jit(solution)/shard_map/reduce_scatter | solution.py:204
  1353.0 153.9 %all-reduce.18.cloned.1.call-done = (bf16[256,2048]{1,0:T(8,128)(2,1)}, bf16[256,2048]{1,0:T(8,128)(2,1)}, bf16[256,2048]{1,0:T(8,128)(2,1)}, bf16[256,2048]{1,0:T(8,128)(2,1)}) async-done(((bf16[256,2048]{1,0:T(8,128)(2,1)}, bf16[256,2048]{1,0:T(8,128)(2,1)}, bf16[256,2048]{1,0:T(8,128)(2,1)}, bf16[256,2048]{1,0:T(8,128)(2,1)}), (bf16[256,2048]{1,0:T(8,128)(2,1)}, bf16[256,2048]{1,0:T(8,128)(2,1)}, ...) | async-done | bytes 4194320 | tf_op jit(solution)/shard_map/psum | solution.py:294
  1515.8 273.0 %reduce-scatter.15.cloned.1.call-done = bf16[2,512,2048]{2,1,0:T(8,128)(2,1)} async-done(((bf16[2,2048,2048]{2,1,0:T(8,128)(2,1)}), bf16[2,512,2048]{2,1,0:T(8,128)(2,1)}) %reduce-scatter.15.cloned.1.call-update) | async-done | bytes 4194320 | tf_op jit(solution)/shard_map/reduce_scatter | solution.py:201
  (346 shorter events, 441.4 us)
Async XLA Ops:
  7.3 135.6 %all-gather.9.cloned.1.call-start = ((), (), s32[]{:S(2)}) async-start(), calls=%async_computation.17 | async-start | bytes 9437184 | tf_op jit(solution)/shard_map/all_gather | solution.py:95
  8.0 146.8 %all-gather.11.cloned.1.call-start = ((), (), s32[]{:S(2)}) async-start(), calls=%async_computation.18 | async-start | bytes 9437184 | tf_op jit(solution)/shard_map/all_gather | solution.py:96
  8.7 246.3 %all-gather.7.cloned.1.call-start = ((), (), s32[]{:S(2)}) async-start(), calls=%async_computation.16 | async-start | bytes 9437184 | tf_op jit(solution)/shard_map/all_gather | solution.py:97
  9.5 320.0 %all-gather.13.cloned.1.call-start = ((), (), s32[]{:S(2)}) async-start(), calls=%async_computation.19 | async-start | bytes 9437184 | tf_op jit(solution)/shard_map/all_gather | solution.py:98
  10.7 9.8 all-to-all-start.1
  17.9 311.6 %copy-start.59 = (f32[256]{0:T(256)}, f32[256]{0:T(256)S(1)}, u32[]{:S(2)}) copy-start(f32[256]{0:T(256)S(1)} %compare_convert_fusion) | copy-start | bytes 3076
  20.6 38.4 %all-to-all-start.2 = ((s32[8,1,256]{2,1,0:T(1,128)}), s32[8,1,256]{2,1,0:T(1,128)S(1)}, u32[]{:S(2)}, u32[]{:S(2)}) async-start(s32[8,1,256]{2,1,0:T(1,128)} %reshape.509), calls=%async_computation.2 | async-start | bytes 16384 | tf_op jit(solution)/shard_map/all_to_all | solution.py:85
  58.5 286.5 %copy-start.47 = (f32[8,1,256]{2,1,0:T(1,128)}, f32[8,1,256]{2,1,0:T(1,128)S(1)}, u32[]{:S(2)}) copy-start(f32[8,1,256]{2,1,0:T(1,128)S(1)} %convert_element_type.304) | copy-start | bytes 24580
  59.0 18.9 %all-to-all-start = ((bf16[8,32,2048]{2,1,0:T(8,128)(2,1)}), bf16[8,32,2048]{2,1,0:T(8,128)(2,1)S(1)}, u32[]{:S(2)}, u32[]{:S(2)}) async-start(bf16[8,32,2048]{2,1,0:T(8,128)(2,1)} %param.15), calls=%async_computation | async-start | bytes 2097152 | tf_op jit(solution)/shard_map/all_to_all | solution.py:78
  77.9 251.6 %copy-start.3 = (bf16[8,32,2048]{2,1,0:T(8,128)(2,1)}, bf16[8,32,2048]{2,1,0:T(8,128)(2,1)S(1)}, u32[]{:S(2)}) copy-start(bf16[8,32,2048]{2,1,0:T(8,128)(2,1)S(1)} %all-to-all-done) | copy-start | bytes 3145732
  77.9 36.2 %all-to-all-start.6 = ((bf16[8,32,2048]{2,1,0:T(8,128)(2,1)}), bf16[8,32,2048]{2,1,0:T(8,128)(2,1)}, u32[]{:S(2)}, u32[]{:S(2)}) async-start(bf16[8,32,2048]{2,1,0:T(8,128)(2,1)} %param.16), calls=%async_computation.6 | async-start | bytes 2097152 | tf_op jit(solution)/shard_map/all_to_all | solution.py:79
  137.1 227.2 %all-to-all-start.7 = ((bf16[8,2,144,2048]{3,2,1,0:T(8,128)(2,1)}), bf16[8,2,144,2048]{3,2,1,0:T(8,128)(2,1)}, u32[]{:S(2)}, u32[]{:S(2)}) async-start(bf16[8,2,144,2048]{3,2,1,0:T(8,128)(2,1)} %multiply_convert_fusion), calls=%async_computation.7 | async-start | bytes 18874368 | tf_op jit(solution)/shard_map/all_to_all | solution.py:186
  364.3 110.4 %all-to-all-start.3 = ((bf16[8,2,144,2048]{3,2,1,0:T(8,128)(2,1)}), bf16[8,2,144,2048]{3,2,1,0:T(8,128)(2,1)}, u32[]{:S(2)}, u32[]{:S(2)}) async-start(bf16[8,2,144,2048]{3,2,1,0:T(8,128)(2,1)} %broadcast_multiply_fusion), calls=%async_computation.3 | async-start | bytes 18874368 | tf_op jit(solution)/shard_map/all_to_all | solution.py:167
  581.4 110.4 %all-to-all-start.4 = ((bf16[1,2,1152,2048]{3,1,0,2:T(2,128)(2,1)}), bf16[1,2,1152,2048]{3,1,0,2:T(2,128)(2,1)}, u32[]{:S(2)}, u32[]{:S(2)}) async-start(bf16[1,2,1152,2048]{3,1,0,2:T(2,128)(2,1)} %copy.113), calls=%async_computation.4 | async-start | bytes 18874368 | tf_op jit(solution)/shard_map/all_to_all | solution.py:178
  691.8 110.3 %all-to-all-start.8 = ((bf16[1,2,1152,2048]{3,1,0,2:T(2,128)(2,1)}), bf16[1,2,1152,2048]{3,1,0,2:T(2,128)(2,1)}, u32[]{:S(2)}, u32[]{:S(2)}) async-start(bf16[1,2,1152,2048]{3,1,0,2:T(2,128)(2,1)} %copy.119), calls=%async_computation.8 | async-start | bytes 18874368 | tf_op jit(solution)/shard_map/all_to_all | solution.py:208
  696.8 279.3 %reduce-scatter.11.cloned.1.call-start = ((), (), s32[]{:S(2)}) async-start(), calls=%async_computation.22 | async-start | bytes 9437184 | tf_op jit(solution)/shard_map/reduce_scatter | solution.py:274
  905.3 145.7 %reduce-scatter.13.cloned.1.call-start = ((), (), s32[]{:S(2)}) async-start(), calls=%async_computation.23 | async-start | bytes 9437184 | tf_op jit(solution)/shard_map/reduce_scatter | solution.py:277
  914.6 211.4 %reduce-scatter.9.cloned.1.call-start = ((), (), s32[]{:S(2)}) async-start(), calls=%async_computation.21 | async-start | bytes 9437184 | tf_op jit(solution)/shard_map/reduce_scatter | solution.py:271
  937.6 264.0 %reduce-scatter.7.cloned.1.call-start = ((), (), s32[]{:S(2)}) async-start(), calls=%async_computation.20 | async-start | bytes 9437184 | tf_op jit(solution)/shard_map/reduce_scatter | solution.py:268
  947.3 401.6 %reduce-scatter.17.cloned.1.call-start = ((), (), s32[]{:S(2)}) async-start(), calls=%async_computation.25 | async-start | bytes 10485760 | tf_op jit(solution)/shard_map/reduce_scatter | solution.py:204
  965.3 541.7 %all-reduce.18.cloned.1.call-start = ((), (), s32[]{:S(2)}) async-start(), calls=%async_computation.26 | async-start | bytes 8388608 | tf_op jit(solution)/shard_map/psum | solution.py:294
  1201.6 587.2 %reduce-scatter.15.cloned.1.call-start = ((), (), s32[]{:S(2)}) async-start(), calls=%async_computation.24 | async-start | bytes 20971520 | tf_op jit(solution)/shard_map/reduce_scatter | solution.py:201
  1260.5 19.6 %all-to-all-start.9 = ((bf16[8,2,32768]{2,1,0:T(2,128)(2,1)}), bf16[8,2,32768]{2,1,0:T(2,128)(2,1)}, u32[]{:S(2)}, u32[]{:S(2)}) async-start(bf16[8,2,32768]{2,1,0:T(2,128)(2,1)} %reshape.515), calls=%async_computation.9 | async-start | bytes 2097152 | tf_op jit(solution)/shard_map/all_to_all | solution.py:265
  1280.2 46.8 %all-to-all-start.5 = ((bf16[8,2,32768]{2,1,0:T(2,128)(2,1)}), bf16[8,2,32768]{2,1,0:T(2,128)(2,1)S(1)}, u32[]{:S(2)}, u32[]{:S(2)}) async-start(bf16[8,2,32768]{2,1,0:T(2,128)(2,1)} %reshape.513), calls=%async_computation.5 | async-start | bytes 2097152 | tf_op jit(solution)/shard_map/all_to_all | solution.py:262
  (77 other events, 1442.0 us)
Sparse Core Ops, SparseCore 0:
  9.9 57.3 all-gather.8
  69.2 65.4 all-gather.10
  136.5 118.4 all-gather.6
  256.7 72.6 all-gather.12
  905.4 70.6 reduce-scatter.10
  979.5 71.5 reduce-scatter.12
  1054.5 71.5 reduce-scatter.8
  1130.1 71.4 reduce-scatter.6
  1204.0 144.8 reduce-scatter.16
  1351.3 155.5 all-reduce.17
  1509.3 279.4 reduce-scatter.14
where the time goes:
time: 1810 us; the launch traced here: 1800 us
  waiting for transfers between devices  1090 us (60%)
  local copies, waits for them, and re-layouts  247 us (14%)
  matrix products  231 us (13%)
  other arithmetic  106 us (6%)
  blocking collectives  66.2 us (4%)
  starting transfers between devices  45.7 us (3%)
  between operations  18.4 us (1%)
    reduce_scatter x1, waiting for transfers between devices, shards(): lax.psum_scatter(in_local_grad.astype(jnp.bfloat16), 'rep', scatter_dimen...  273 us
    psum x1, waiting for transfers between devices, shards(): lax.psum(shares[0].astype(jnp.bfloat16), 'rep').astype(jnp.float32)  154 us
    all_to_all x1, waiting for transfers between devices, shards(): lax.all_to_all(outgoing, 'ep', split_axis=0, concat_axis=2, tiled=True)[0]  96.1 us
    all_to_all x1, waiting for transfers between devices, shards(): lax.all_to_all(arrived_back[None], 'ep', split_axis=2, concat_axis=0, til...  93.1 us
    reduce_scatter x1, waiting for transfers between devices, shards(): lax.psum_scatter(query_weight_grad.astype(jnp.bfloat16), 'ep', scatter_di...  75.6 us
    reduce_scatter x1, waiting for transfers between devices, shards(): lax.psum_scatter(key_weight_grad.astype(jnp.bfloat16), 'ep', scatter_dime...  75 us
    reduce_scatter x1, waiting for transfers between devices, shards(): lax.psum_scatter(output_weight_grad.astype(jnp.bfloat16), 'ep', scatter_d...  74.9 us
    all_gather x1, waiting for transfers between devices, shards(): lax.all_gather(value_weight, 'ep', axis=0, tiled=True)  71.8 us
  transfers between devices with their start and end apart: 21, of which 15 were waited for; matrix products, arithmetic and copies ran while one was open for 20% of the time, Pallas kernels for 0%

commit v1 on v0

--- a/solution.py
+++ b/solution.py
@@ -291,7 +291,7 @@
         ).astype(jnp.float32),
     )
     shares = (
-        lax.psum(shares[0].astype(jnp.bfloat16), "rep").astype(jnp.float32),
+        jnp.sum(lax.all_gather(shares[0].astype(jnp.bfloat16), "rep"), axis=0).astype(jnp.float32),
         lax.psum(shares[1].astype(jnp.bfloat16), "rep").astype(jnp.float32),
         lax.psum(shares[2].astype(jnp.bfloat16), "rep").astype(jnp.float32),
         lax.psum(shares[3].astype(jnp.bfloat16), "rep").astype(jnp.float32),

time: 1810 us -> 1860 us (1.028)
  waiting for transfers between devices: 1090 us -> 1130 us
    all_gather x0 -> x1, waiting for transfers between devices: none -> 74.1 us  [shards(): lax.all_gather(shares[0].astype(jnp.bfloat16), 'rep')]
    psum x1, waiting for transfers between devices: 154 us -> 120 us  [shards(): lax.psum(shares[1].astype(jnp.bfloat16), 'rep').astype(jnp.float32)]
  transfers between devices with their start and end apart: 21 -> 22, of which waited for: 15 -> 16; matrix products, arithmetic and copies ran while one was open for 20% -> 19% of each run, Pallas kernels for 0% -> 0%
where the time goes in v1:
time: 1860 us; the launch traced here: 1850 us
  waiting for transfers between devices  1130 us (61%)
  local copies, waits for them, and re-layouts  247 us (13%)
  matrix products  231 us (12%)
  other arithmetic  109 us (6%)
  blocking collectives  66.2 us (4%)
  starting transfers between devices  45.7 us (2%)
  between operations  18.7 us (1%)
    reduce_scatter x1, waiting for transfers between devices, shards(): lax.psum_scatter(in_local_grad.astype(jnp.bfloat16), 'rep', scatter_dimen...  277 us
    psum x1, waiting for transfers between devices, shards(): lax.psum(shares[1].astype(jnp.bfloat16), 'rep').astype(jnp.float32)  120 us
    all_to_all x1, waiting for transfers between devices, shards(): lax.all_to_all(outgoing, 'ep', split_axis=0, concat_axis=2, tiled=True)[0]  96.1 us
    all_to_all x1, waiting for transfers between devices, shards(): lax.all_to_all(arrived_back[None], 'ep', split_axis=2, concat_axis=0, til...  93.1 us
    reduce_scatter x1, waiting for transfers between devices, shards(): lax.psum_scatter(query_weight_grad.astype(jnp.bfloat16), 'ep', scatter_di...  75.5 us
    reduce_scatter x1, waiting for transfers between devices, shards(): lax.psum_scatter(key_weight_grad.astype(jnp.bfloat16), 'ep', scatter_dime...  75 us
    reduce_scatter x1, waiting for transfers between devices, shards(): lax.psum_scatter(output_weight_grad.astype(jnp.bfloat16), 'ep', scatter_d...  74.9 us
    all_gather x1, waiting for transfers between devices, shards(): lax.all_gather(shares[0].astype(jnp.bfloat16), 'rep')  74.1 us
  transfers between devices with their start and end apart: 22, of which 16 were waited for; matrix products, arithmetic and copies ran while one was open for 19% of the time, Pallas kernels for 0%

profile of v1, /device:TPU:0, one launch (start us, length us, event | category | flops | bytes accessed | tf_op | source)
XLA Modules:
  0.0 1849.4 jit_solution(13538061019130395784)
XLA Ops:
  183.3 71.7 %all-gather.9.cloned.1.call-done = bf16[2048,2048]{1,0:T(8,128)(2,1)} async-done(((bf16[256,2048]{1,0:T(8,128)(2,1)}), bf16[2048,2048]{1,0:T(8,128)(2,1)}) %all-gather.9.cloned.1.call-update) | async-done | bytes 8388624 | tf_op jit(solution)/shard_map/all_gather | solution.py:97
  263.1 66.4 %all-gather.15.cloned.1.call-done = bf16[2048,2048]{1,0:T(8,128)(2,1)} async-done(((bf16[256,2048]{1,0:T(8,128)(2,1)}), bf16[2048,2048]{1,0:T(8,128)(2,1)}) %all-gather.15.cloned.1.call-update) | async-done | bytes 8388624 | tf_op jit(solution)/shard_map/all_gather | solution.py:98
  329.5 15.5 multiply_reduce_fusion.7
  378.7 96.1 %all-to-all-done.3 = bf16[8,2,144,2048]{3,2,1,0:T(8,128)(2,1)} async-done(((bf16[8,2,144,2048]{3,2,1,0:T(8,128)(2,1)}), bf16[8,2,144,2048]{3,2,1,0:T(8,128)(2,1)}, u32[]{:S(2)}, u32[]{:S(2)}) %all-to-all-start.3) | async-done | bytes 9437216 | tf_op jit(solution)/shard_map/all_to_all | solution.py:167
  484.0 27.3 %fusion.66 = f32[2,1152,2048]{2,1,0:T(8,128)} fusion(bf16[2,1152,2048]{2,1,0:T(8,128)(2,1)} %bitcast.189, bf16[2,2048,2048]{2,1,0:T(8,128)(2,1)} %param.28), kind=kOutput, calls=%fused_computation.165 | convolution fusion | flops 19327352832 | bytes 45088768 | tf_op jit(solution)/shard_map/erd,edf->erf/dot_general | solution.py:168
  511.3 27.5 %fusion.31 = (f32[2,1152,1024]{2,1,0:T(8,128)}, f32[2,1152,1024]{2,1,0:T(8,128)}, bf16[2,1152,1024]{2,1,0:T(8,128)(2,1)}) fusion(f32[2,1152,2048]{2,1,0:T(8,128)} %fusion.66, bf16[2,1152,2048]{2,1,0:T(8,128)(2,1)} %bitcast.191, bf16[2,1024,2048]{2,1,0:T(8,128)(2,1)} %param.29), kind=kOutput, calls=%fused_computation.95 | convolution fusion | flops 9696706560 | bytes 60293120 | tf_op jit(solution)/shard_map/erd,efd->erf/dot_general | solution.py:187
  538.8 14.6 fusion.4
  553.4 27.9 %copy.113 = bf16[1,2,1152,2048]{3,1,0,2:T(2,128)(2,1)} copy(bf16[1,2,1152,2048]{3,2,1,0:T(8,128)(2,1)S(1)} %fusion.4) | data formatting | bytes 18874368 | tf_op jit(solution)/shard_map/broadcast_in_dim | solution.py:179
  586.5 27.6 %fusion.5 = bf16[1,2,1152,2048]{3,2,1,0:T(8,128)(2,1)} fusion(bf16[2,2048,2048]{2,1,0:T(8,128)(2,1)} %param.28, f32[2,1152,1024]{2,1,0:T(8,128)} %get-tuple-element.36, f32[2,1152,1024]{2,1,0:T(8,128)} %get-tuple-element.35), kind=kOutput, calls=%fused_computation.22 | convolution fusion | flops 19341508608 | bytes 45088768 | tf_op jit(solution)/shard_map/erf,edf->erd/dot_general | solution.py:197
  614.1 18.2 copy.119
  632.3 59.4 %all-to-all-done.4 = bf16[1,2,1152,2048]{3,1,0,2:T(2,128)(2,1)} async-done(((bf16[1,2,1152,2048]{3,1,0,2:T(2,128)(2,1)}), bf16[1,2,1152,2048]{3,1,0,2:T(2,128)(2,1)}, u32[]{:S(2)}, u32[]{:S(2)}) %all-to-all-start.4) | async-done | bytes 9437216 | tf_op jit(solution)/shard_map/all_to_all | solution.py:178
  709.0 93.1 %all-to-all-done.8 = bf16[1,2,1152,2048]{3,1,0,2:T(2,128)(2,1)} async-done(((bf16[1,2,1152,2048]{3,1,0,2:T(2,128)(2,1)}), bf16[1,2,1152,2048]{3,1,0,2:T(2,128)(2,1)}, u32[]{:S(2)}, u32[]{:S(2)}) %all-to-all-start.8) | async-done | bytes 9437216 | tf_op jit(solution)/shard_map/all_to_all | solution.py:208
  813.8 21.2 %gather_fusion.1 = bf16[2048,2048]{1,0:T(8,128)(2,1)} fusion(bf16[2304,2048]{1,0:T(8,128)(2,1)} %bitcast.179, s32[2048]{0:T(1024)S(1)} %broadcast_clamp_fusion), kind=kCustom, calls=%fused_computation.1 | custom fusion | bytes 16785408 | tf_op jit(solution)/shard_map/gather | solution.py:181
  835.1 21.4 %gather_fusion.3 = bf16[2048,2048]{1,0:T(8,128)(2,1)} fusion(bf16[2304,2048]{1,0:T(8,128)(2,1)} %bitcast.180, s32[2048]{0:T(1024)S(1)} %broadcast_clamp_fusion), kind=kCustom, calls=%fused_computation.3 | custom fusion | bytes 16785408 | tf_op jit(solution)/shard_map/gather | solution.py:212
  947.4 17.9 convolution_convert_fusion.7
  976.1 74.9 %reduce-scatter.13.cloned.1.call-done = bf16[256,2048]{1,0:T(8,128)(2,1)} async-done(((bf16[2048,2048]{1,0:T(8,128)(2,1)}), bf16[256,2048]{1,0:T(8,128)(2,1)}) %reduce-scatter.13.cloned.1.call-update) | async-done | bytes 1048592 | tf_op jit(solution)/shard_map/reduce_scatter | solution.py:277
  1050.9 75.0 %reduce-scatter.9.cloned.1.call-done = bf16[256,2048]{1,0:T(8,128)(2,1)} async-done(((bf16[2048,2048]{1,0:T(8,128)(2,1)}), bf16[256,2048]{1,0:T(8,128)(2,1)}) %reduce-scatter.9.cloned.1.call-update) | async-done | bytes 1048592 | tf_op jit(solution)/shard_map/reduce_scatter | solution.py:271
  1126.0 75.5 %reduce-scatter.7.cloned.1.call-done = bf16[256,2048]{1,0:T(8,128)(2,1)} async-done(((bf16[2048,2048]{1,0:T(8,128)(2,1)}), bf16[256,2048]{1,0:T(8,128)(2,1)}) %reduce-scatter.7.cloned.1.call-update) | async-done | bytes 1048592 | tf_op jit(solution)/shard_map/reduce_scatter | solution.py:268
  1201.6 29.3 %convolution_convert_fusion = bf16[2,2048,2048]{2,1,0:T(8,128)(2,1)} fusion(bf16[2,1152,2048]{2,1,0:T(8,128)(2,1)} %bitcast.190, f32[2,1152,1024]{2,1,0:T(8,128)} %get-tuple-element.36, f32[2,1152,1024]{2,1,0:T(8,128)} %get-tuple-element.35), kind=kOutput, calls=%fused_computation.13 | convolution fusion | flops 19345178624 | bytes 45088768 | tf_op jit(solution)/shard_map/erd,erf->edf/dot_general | solution.py:194
  1285.0 21.1 %all-reduce.12 = (bf16[2048]{0:T(1024)(128)(2,1)S(1)}, bf16[2048]{0:T(1024)(128)(2,1)S(1)}, bf16[128]{0:T(256)(128)(2,1)S(1)}, bf16[128]{0:T(256)(128)(2,1)S(1)}) all-reduce(bf16[2048]{0:T(1024)(128)(2,1)S(1)} %get-tuple-element.18, bf16[2048]{0:T(1024)(128)(2,1)S(1)} %get-tuple-element.16, ...), channel_id=7, replica_groups=mesh['rep'=4,'ep'=8] {'ep'}, use_global_device_ids=true, to_apply=%region_28.29.clone | all-reduce | flops 4352 | bytes 17408
  1329.5 19.3 %reduce-scatter.17.cloned.1.call-done = bf16[2,256,2048]{2,1,0:T(8,128)(2,1)} async-done(((bf16[2,1024,2048]{2,1,0:T(8,128)(2,1)}), bf16[2,256,2048]{2,1,0:T(8,128)(2,1)}) %reduce-scatter.17.cloned.1.call-update) | async-done | bytes 2097168 | tf_op jit(solution)/shard_map/reduce_scatter | solution.py:204
  1352.9 120.0 %all-reduce.18.cloned.1.call-done = (bf16[256,2048]{1,0:T(8,128)(2,1)}, bf16[256,2048]{1,0:T(8,128)(2,1)}, bf16[256,2048]{1,0:T(8,128)(2,1)}) async-done(((bf16[256,2048]{1,0:T(8,128)(2,1)}, bf16[256,2048]{1,0:T(8,128)(2,1)}, bf16[256,2048]{1,0:T(8,128)(2,1)}), (bf16[256,2048]{1,0:T(8,128)(2,1)}, bf16[256,2048]{1,0:T(8,128)(2,1)}, bf16[256,2048]{1,0:T(8,128)(2,1)})) %all-reduce.18.cloned.1.call-update) | async-done | bytes 3145744 | tf_op jit(solution)/shard_map/psum | solution.py:295
  1480.1 74.1 %all-gather.17.cloned.1.call-done = bf16[1024,2048]{1,0:T(8,128)(2,1)} async-done(((bf16[256,2048]{1,0:T(8,128)(2,1)}), bf16[1024,2048]{1,0:T(8,128)(2,1)}) %all-gather.17.cloned.1.call-update) | async-done | bytes 4194320 | tf_op jit(solution)/shard_map/all_gather | solution.py:294
  1558.9 276.5 %reduce-scatter.15.cloned.1.call-done = bf16[2,512,2048]{2,1,0:T(8,128)(2,1)} async-done(((bf16[2,2048,2048]{2,1,0:T(8,128)(2,1)}), bf16[2,512,2048]{2,1,0:T(8,128)(2,1)}) %reduce-scatter.15.cloned.1.call-update) | async-done | bytes 4194320 | tf_op jit(solution)/shard_map/reduce_scatter | solution.py:201
  (348 shorter events, 459.1 us)
Async XLA Ops:
  7.3 135.6 %all-gather.11.cloned.1.call-start = ((), (), s32[]{:S(2)}) async-start(), calls=%async_computation.17 | async-start | bytes 9437184 | tf_op jit(solution)/shard_map/all_gather | solution.py:95
  8.0 146.9 %all-gather.13.cloned.1.call-start = ((), (), s32[]{:S(2)}) async-start(), calls=%async_computation.18 | async-start | bytes 9437184 | tf_op jit(solution)/shard_map/all_gather | solution.py:96
  8.7 246.3 %all-gather.9.cloned.1.call-start = ((), (), s32[]{:S(2)}) async-start(), calls=%async_computation.16 | async-start | bytes 9437184 | tf_op jit(solution)/shard_map/all_gather | solution.py:97
  9.5 320.0 %all-gather.15.cloned.1.call-start = ((), (), s32[]{:S(2)}) async-start(), calls=%async_computation.19 | async-start | bytes 9437184 | tf_op jit(solution)/shard_map/all_gather | solution.py:98
  10.7 9.8 all-to-all-start.1
  17.9 311.6 %copy-start.58 = (f32[256]{0:T(256)}, f32[256]{0:T(256)S(1)}, u32[]{:S(2)}) copy-start(f32[256]{0:T(256)S(1)} %compare_convert_fusion) | copy-start | bytes 3076
  20.6 38.4 %all-to-all-start.2 = ((s32[8,1,256]{2,1,0:T(1,128)}), s32[8,1,256]{2,1,0:T(1,128)S(1)}, u32[]{:S(2)}, u32[]{:S(2)}) async-start(s32[8,1,256]{2,1,0:T(1,128)} %reshape.510), calls=%async_computation.2 | async-start | bytes 16384 | tf_op jit(solution)/shard_map/all_to_all | solution.py:85
  58.5 286.5 %copy-start.46 = (f32[8,1,256]{2,1,0:T(1,128)}, f32[8,1,256]{2,1,0:T(1,128)S(1)}, u32[]{:S(2)}) copy-start(f32[8,1,256]{2,1,0:T(1,128)S(1)} %convert_element_type.306) | copy-start | bytes 24580
  59.0 18.9 %all-to-all-start = ((bf16[8,32,2048]{2,1,0:T(8,128)(2,1)}), bf16[8,32,2048]{2,1,0:T(8,128)(2,1)S(1)}, u32[]{:S(2)}, u32[]{:S(2)}) async-start(bf16[8,32,2048]{2,1,0:T(8,128)(2,1)} %param.15), calls=%async_computation | async-start | bytes 2097152 | tf_op jit(solution)/shard_map/all_to_all | solution.py:78
  77.9 36.2 %all-to-all-start.6 = ((bf16[8,32,2048]{2,1,0:T(8,128)(2,1)}), bf16[8,32,2048]{2,1,0:T(8,128)(2,1)}, u32[]{:S(2)}, u32[]{:S(2)}) async-start(bf16[8,32,2048]{2,1,0:T(8,128)(2,1)} %param.16), calls=%async_computation.6 | async-start | bytes 2097152 | tf_op jit(solution)/shard_map/all_to_all | solution.py:79
  137.1 227.3 %all-to-all-start.7 = ((bf16[8,2,144,2048]{3,2,1,0:T(8,128)(2,1)}), bf16[8,2,144,2048]{3,2,1,0:T(8,128)(2,1)}, u32[]{:S(2)}, u32[]{:S(2)}) async-start(bf16[8,2,144,2048]{3,2,1,0:T(8,128)(2,1)} %multiply_convert_fusion), calls=%async_computation.7 | async-start | bytes 18874368 | tf_op jit(solution)/shard_map/all_to_all | solution.py:186
  364.4 110.4 %all-to-all-start.3 = ((bf16[8,2,144,2048]{3,2,1,0:T(8,128)(2,1)}), bf16[8,2,144,2048]{3,2,1,0:T(8,128)(2,1)}, u32[]{:S(2)}, u32[]{:S(2)}) async-start(bf16[8,2,144,2048]{3,2,1,0:T(8,128)(2,1)} %broadcast_multiply_fusion), calls=%async_computation.3 | async-start | bytes 18874368 | tf_op jit(solution)/shard_map/all_to_all | solution.py:167
  581.4 110.4 %all-to-all-start.4 = ((bf16[1,2,1152,2048]{3,1,0,2:T(2,128)(2,1)}), bf16[1,2,1152,2048]{3,1,0,2:T(2,128)(2,1)}, u32[]{:S(2)}, u32[]{:S(2)}) async-start(bf16[1,2,1152,2048]{3,1,0,2:T(2,128)(2,1)} %copy.113), calls=%async_computation.4 | async-start | bytes 18874368 | tf_op jit(solution)/shard_map/all_to_all | solution.py:178
  691.7 110.3 %all-to-all-start.8 = ((bf16[1,2,1152,2048]{3,1,0,2:T(2,128)(2,1)}), bf16[1,2,1152,2048]{3,1,0,2:T(2,128)(2,1)}, u32[]{:S(2)}, u32[]{:S(2)}) async-start(bf16[1,2,1152,2048]{3,1,0,2:T(2,128)(2,1)} %copy.119), calls=%async_computation.8 | async-start | bytes 18874368 | tf_op jit(solution)/shard_map/all_to_all | solution.py:208
  696.8 279.3 %reduce-scatter.11.cloned.1.call-start = ((), (), s32[]{:S(2)}) async-start(), calls=%async_computation.22 | async-start | bytes 9437184 | tf_op jit(solution)/shard_map/reduce_scatter | solution.py:274
  905.3 145.6 %reduce-scatter.13.cloned.1.call-start = ((), (), s32[]{:S(2)}) async-start(), calls=%async_computation.23 | async-start | bytes 9437184 | tf_op jit(solution)/shard_map/reduce_scatter | solution.py:277
  914.6 211.3 %reduce-scatter.9.cloned.1.call-start = ((), (), s32[]{:S(2)}) async-start(), calls=%async_computation.21 | async-start | bytes 9437184 | tf_op jit(solution)/shard_map/reduce_scatter | solution.py:271
  937.5 264.0 %reduce-scatter.7.cloned.1.call-start = ((), (), s32[]{:S(2)}) async-start(), calls=%async_computation.20 | async-start | bytes 9437184 | tf_op jit(solution)/shard_map/reduce_scatter | solution.py:268
  947.3 401.5 %reduce-scatter.17.cloned.1.call-start = ((), (), s32[]{:S(2)}) async-start(), calls=%async_computation.25 | async-start | bytes 10485760 | tf_op jit(solution)/shard_map/reduce_scatter | solution.py:204
  965.2 507.7 %all-reduce.18.cloned.1.call-start = ((), (), s32[]{:S(2)}) async-start(), calls=%async_computation.27 | async-start | bytes 6291456 | tf_op jit(solution)/shard_map/psum | solution.py:295
  1126.0 428.3 %all-gather.17.cloned.1.call-start = ((), (), s32[]{:S(2)}) async-start(), calls=%async_computation.26 | async-start | bytes 5242880 | tf_op jit(solution)/shard_map/all_gather | solution.py:294
  1201.6 633.9 %reduce-scatter.15.cloned.1.call-start = ((), (), s32[]{:S(2)}) async-start(), calls=%async_computation.24 | async-start | bytes 20971520 | tf_op jit(solution)/shard_map/reduce_scatter | solution.py:201
  1260.5 19.6 %all-to-all-start.9 = ((bf16[8,2,32768]{2,1,0:T(2,128)(2,1)}), bf16[8,2,32768]{2,1,0:T(2,128)(2,1)}, u32[]{:S(2)}, u32[]{:S(2)}) async-start(bf16[8,2,32768]{2,1,0:T(2,128)(2,1)} %reshape.516), calls=%async_computation.9 | async-start | bytes 2097152 | tf_op jit(solution)/shard_map/all_to_all | solution.py:265
  1280.1 46.8 %all-to-all-start.5 = ((bf16[8,2,32768]{2,1,0:T(2,128)(2,1)}), bf16[8,2,32768]{2,1,0:T(2,128)(2,1)S(1)}, u32[]{:S(2)}, u32[]{:S(2)}) async-start(bf16[8,2,32768]{2,1,0:T(2,128)(2,1)} %reshape.514), calls=%async_computation.5 | async-start | bytes 2097152 | tf_op jit(solution)/shard_map/all_to_all | solution.py:262
  (77 other events, 1686.4 us)
Sparse Core Ops, SparseCore 0:
  9.9 57.3 all-gather.10
  69.2 65.4 all-gather.12
  136.5 118.4 all-gather.8
  256.8 72.6 all-gather.14
  905.4 70.6 reduce-scatter.10
  979.4 71.5 reduce-scatter.12
  1054.4 71.5 reduce-scatter.8
  1130.0 71.5 reduce-scatter.6
  1203.9 144.8 reduce-scatter.16
  1351.2 121.6 all-reduce.17
  1474.5 79.7 all-gather.16
  1556.5 278.9 reduce-scatter.14
